TPU v7x, 256 devices: a whole 4x4x8 slice. The times are simulated.
256 devices in a mesh: ctx: 16 (over z_hi, x, core), exp: 16 (over y, z_lo).
Axes of the slice: x: 4, y: 4, z: 8 (z_hi: 2, z_lo: 4; z = z_hi * 4 + z_lo), core: 2. Of those that a mesh axis runs over, the one named last changes fastest.
Arguments:
- q_nope: bfloat16 [1024, 128, 512], P('ctx', 'exp'), may hold values from -72 to 72
- q_rope: bfloat16 [1024, 8192], P('ctx', 'exp'), may hold values from -6 to 6
- cache_keys: bfloat16 [576, 2048], P(None, 'ctx'), may hold values from -6 to 6
- fresh_keys: bfloat16 [576, 1024], P(None, 'ctx'), may hold values from -6 to 6
- block_order: int32 [32], replicated, may hold values from 0 to 31, each once
- w_uv: bfloat16 [128, 512, 128], P('exp'), may hold values from -0.25 to 0.25
- w_out: bfloat16 [16384, 7168], P('exp', 'ctx'), may hold values from -0.046875 to 0.046875
- residual: bfloat16 [1024, 7168], P(('ctx', 'exp')), may hold values from -6 to 6
- norm_gain: float32 [7168], replicated, may hold values from 0.5 to 1.5
- router_weight: bfloat16 [7168, 16], replicated, may hold values from -0.0625 to 0.0625
- expert_ids: int32 [1024, 8], P(('ctx', 'exp')), may hold values from 0 to 15, all different within a row; in each aligned block of 4 rows (0 to 3, 4 to 7, ...) at most 3 rows name the same one
- w_gate: bfloat16 [16, 7168, 2048], P('exp', None, 'ctx'), may hold values from -0.0625 to 0.0625
- w_up: bfloat16 [16, 7168, 2048], P('exp', None, 'ctx'), may hold values from -0.0625 to 0.0625
- w_down: bfloat16 [16, 2048, 7168], P('exp', 'ctx'), may hold values from -0.125 to 0.125
Outputs:
- layer_out: bfloat16 [1024, 7168], P(('ctx', 'exp'))
Inputs may be any that keep to these rules, and one draw needn't show every extreme that they name: A permutation: block j of the new tokens (32 rows) sits at positions 2048 + block_order[j] * 32 onward. `expert_ids`: each row names 8 different experts; the 4 rows of one device name no expert more than 3 times, and in some aligned block one expert exactly 3 times.
All inputs are finite; a program needn't handle non-finite values.
Results may differ from a plain program's by a relative error of at most 0.012.
Values may be sent and summed in bfloat16 or wider, within the bound.
A program may use at most 128 MiB of HBM per device.

v0:
```python
import math
import jax
import jax.numpy as jnp
from jax import lax
from jax.sharding import PartitionSpec as P

QKD = 192
CAP = 3
ROUTE_SCALE = 2.5
NORM_EPS = 1e-06


def copy_for_each(value, axis):
    copies = jnp.broadcast_to(value, (lax.axis_size(axis), *value.shape))
    return lax.all_to_all(copies, axis, split_axis=0, concat_axis=0, tiled=True)


def in_order(pieces, dim):
    pieces = jnp.moveaxis(pieces, 0, dim)
    shape = pieces.shape
    return pieces.reshape(*shape[:dim], shape[dim] * shape[dim + 1], *shape[dim + 2 :])


def gather_directly(value, axis, dim):
    pieces = copy_for_each(value, axis)
    return in_order(pieces, dim)


def in_blocks(value, dim, length):
    shape = value.shape
    pieces = value.reshape(*shape[:dim], length, shape[dim] // length, *shape[dim + 1 :])
    return jnp.moveaxis(pieces, dim, 0)


def sum_at_owner(value, axis, dim):
    length = lax.axis_size(axis)
    pieces = lax.all_to_all(in_blocks(value, dim, length), axis, 0, 0, tiled=True)
    return jnp.sum(pieces.astype(jnp.float32), axis=0)


def block_position(row_index, block_order, block_rows):
    blocks = row_index // block_rows
    lookup = blocks[:, None] == jnp.arange(block_order.shape[0], dtype=jnp.int32)[None, :]
    leading = jnp.sum(jnp.where(lookup, block_order[None, :], 0), axis=1)
    return leading * block_rows + row_index % block_rows


def attend(query_lat, query_pe, keys, visible):
    row_count, head_count, latent_width = query_lat.shape
    key_count = keys.shape[1]
    pe_width = query_pe.shape[1] // head_count
    first_dot = jnp.dot(
        query_lat.reshape(row_count * head_count, latent_width),
        keys[:latent_width],
        preferred_element_type=jnp.float32,
    )
    second_dot = jnp.dot(
        query_pe.reshape(row_count * head_count, pe_width),
        keys[latent_width:],
        preferred_element_type=jnp.float32,
    )
    scores = ((first_dot + second_dot) * (1.0 / math.sqrt(QKD))).reshape(
        row_count, head_count, key_count
    )
    scores = jnp.where(visible[:, None, :], scores, -jnp.inf)
    row_max = jnp.max(scores, axis=2)
    exponent = jnp.exp(scores - row_max[:, :, None])
    row_sum = jnp.sum(exponent, axis=2)
    weights = exponent.astype(jnp.bfloat16).reshape(row_count * head_count, key_count)
    latent = lax.dot_general(
        weights, keys[:latent_width], (((1,), (1,)), ((), ())), preferred_element_type=jnp.float32
    )
    return (row_max, row_sum, latent.reshape(row_count, head_count, latent_width))


def merge_partial(earlier, latter):
    highest = latter[0]
    earlier_scale = jnp.exp(earlier[0] - highest)
    latter_scale = jnp.exp(latter[0] - highest)
    row_sum = earlier_scale * earlier[1] + latter_scale * latter[1]
    latent = earlier_scale[:, :, None] * earlier[2] + latter_scale[:, :, None] * latter[2]
    return (highest, row_sum, latent)


def body(
    q_nope,
    q_rope,
    cache_keys,
    fresh_keys,
    block_order,
    w_uv,
    w_out,
    residual,
    norm_gain,
    router_weight,
    expert_ids,
    w_gate,
    w_up,
    w_down,
):
    ctx_count = lax.axis_size("ctx")
    exp_count = lax.axis_size("exp")
    ctx_index = lax.axis_index("ctx")
    rows_here, heads_here, latent_width = q_nope.shape
    value_width = w_uv.shape[2]
    cache_len = cache_keys.shape[1]
    key_cols = cache_len + rows_here
    block_rows = rows_here // 2
    keys_here = jnp.concatenate([cache_keys, fresh_keys], axis=1)
    w_uv_wide = w_uv.astype(jnp.float32)
    own_rows = ctx_index * rows_here + jnp.arange(rows_here, dtype=jnp.int32)
    own_pos = block_position(own_rows, block_order, block_rows)
    start_state = (
        jnp.full((rows_here, heads_here), -jnp.inf, jnp.float32),
        jnp.zeros((rows_here, heads_here), jnp.float32),
        jnp.zeros((rows_here, heads_here, latent_width), jnp.float32),
    )
    portion = lax.all_gather(keys_here, "ctx", axis=1, tiled=True)
    columns = jnp.arange(portion.shape[1], dtype=jnp.int32)
    owner_dev = columns // key_cols
    within = columns % key_cols
    fresh_row = owner_dev * rows_here + within - cache_len
    key_pos = jnp.where(within < cache_len, -1, block_position(fresh_row, block_order, block_rows))
    visible = key_pos[None, :] <= own_pos[:, None]
    row_max, row_sum, latent = merge_partial(start_state, attend(q_nope, q_rope, portion, visible))
    normal_lat = latent / row_sum[:, :, None]
    head_wide = jnp.einsum("rhl,hlv->rhv", normal_lat, w_uv_wide, precision=lax.Precision.HIGHEST)
    head_out = head_wide.astype(jnp.bfloat16).reshape(rows_here, heads_here * value_width)
    tok_here, model_width = residual.shape
    col_part = w_out.shape[1]
    head_partial = jnp.dot(
        gather_directly(head_out, "ctx", 0), w_out, preferred_element_type=jnp.float32
    )
    arranged = head_partial.reshape(ctx_count, exp_count, tok_here, col_part)
    head_total = sum_at_owner(arranged.astype(jnp.bfloat16), "exp", 1)
    attention = lax.all_to_all(
        head_total.astype(jnp.bfloat16), "ctx", split_axis=0, concat_axis=3, tiled=True
    ).reshape(tok_here, model_width)
    hidden = residual.astype(jnp.float32) + attention.astype(jnp.float32)
    mean_square = jnp.mean(hidden * hidden, axis=1, keepdims=True)
    normed = (hidden * lax.rsqrt(mean_square + NORM_EPS) * norm_gain).astype(jnp.bfloat16)
    affinity = jax.nn.sigmoid(jnp.dot(normed, router_weight, preferred_element_type=jnp.float32))
    expert_count = router_weight.shape[1]
    onehot = expert_ids[:, :, None] == jnp.arange(expert_count, dtype=jnp.int32)[None, None, :]
    chosen = jnp.sum(jnp.where(onehot, affinity[:, None, :], 0.0), axis=2)
    route = ROUTE_SCALE * chosen / jnp.sum(chosen, axis=1, keepdims=True)
    mixing = jnp.sum(jnp.where(onehot, route[:, :, None], 0.0), axis=1)
    picked = jnp.sum(onehot.astype(jnp.int32), axis=1)
    slot_index = jnp.cumsum(picked, axis=0) - picked
    slot_hot = (slot_index[:, :, None] == jnp.arange(CAP, dtype=jnp.int32)[None, None, :]) & (
        picked[:, :, None] > 0
    )
    dispatch_map = (
        jnp.transpose(slot_hot, (1, 2, 0))
        .reshape(expert_count * CAP, tok_here)
        .astype(jnp.bfloat16)
    )
    send_rows = jnp.dot(dispatch_map, normed, preferred_element_type=jnp.float32).astype(
        jnp.bfloat16
    )
    arrived = lax.all_to_all(
        send_rows.reshape(expert_count, CAP, model_width),
        "exp",
        split_axis=0,
        concat_axis=1,
        tiled=True,
    )
    local_experts = arrived.shape[0]
    portion = lax.all_gather(arrived, "ctx", axis=1, tiled=True)
    gate = jnp.einsum("end,edf->enf", portion, w_gate, preferred_element_type=jnp.float32)
    upward = jnp.einsum("end,edf->enf", portion, w_up, preferred_element_type=jnp.float32)
    activations = (jax.nn.silu(gate) * upward).astype(jnp.bfloat16)
    expert_total = lax.psum_scatter(
        jnp.einsum("enf,efd->ned", activations, w_down, preferred_element_type=jnp.float32).astype(
            jnp.bfloat16
        ),
        "ctx",
        scatter_dimension=0,
        tiled=True,
    )
    going_back = expert_total.reshape(exp_count, CAP, local_experts, model_width)
    returned = lax.all_to_all(going_back, "exp", split_axis=0, concat_axis=2, tiled=True)
    combine_map = jnp.where(slot_hot, mixing[:, :, None], 0.0)
    combine_map = jnp.transpose(combine_map, (0, 2, 1)).reshape(tok_here, CAP * expert_count)
    mixture = jnp.dot(
        combine_map,
        returned.reshape(CAP * expert_count, model_width).astype(jnp.float32),
        precision=lax.Precision.HIGHEST,
    )
    return (hidden + mixture).astype(jnp.bfloat16)


def solution(mesh):
    return jax.shard_map(
        body,
        mesh=mesh,
        in_specs=(
            P("ctx", "exp", None),
            P("ctx", "exp"),
            P(None, "ctx"),
            P(None, "ctx"),
            P(),
            P("exp", None, None),
            P("exp", "ctx"),
            P(("ctx", "exp"), None),
            P(),
            P(),
            P(("ctx", "exp"), None),
            P("exp", None, "ctx"),
            P("exp", None, "ctx"),
            P("exp", "ctx", None),
        ),
        out_specs=P(("ctx", "exp"), None),
        check_vma=False,
    )
```

profile of v0, /device:TPU:1, one launch (start us, length us, event | category | flops | bytes accessed | tf_op | source)
XLA Modules:
  0.0 590.2 jit_solution(14569055627388049429)
XLA Ops:
  6.5 1.2 copy.37
  7.7 1.6 pad_maximum_fusion
  9.4 1.0 reshape.334
  10.4 0.7 select_reduce_fusion.4
  11.1 0.8 select_reduce_fusion
  12.2 77.7 %all-gather.3.cloned.1.call-done = bf16[576,3072]{0,1:T(8,128)(2,1)} async-done(((bf16[576,192]{0,1:T(8,128)(2,1)}), bf16[576,3072]{0,1:T(8,128)(2,1)}) %all-gather.3.cloned.1.call-update) | async-done | bytes 3538960 | tf_op jit(solution)/shard_map/all_gather | solution.py:118
  89.8 3.9 fusion.13
  93.7 3.1 fusion.90
  96.8 2.6 copy-done.1
  99.5 1.0 fusion.6
  100.8 5.6 fusion.37
  106.4 1.2 fusion.56
  108.0 37.4 %all_to_all.46 = bf16[16,64,1024]{2,1,0:T(8,128)(2,1)S(1)} all-to-all(bf16[16,64,1024]{2,1,0:T(8,128)(2,1)S(1)} %broadcast_in_dim.120), channel_id=1, replica_groups=mesh['ctx'=16,'exp'=16] {'ctx'}, dimensions={0} | all-to-all | bytes 4194304 | tf_op jit(solution)/shard_map/all_to_all | solution.py:15
  145.3 1.2 copy.41
  146.5 1.4 fusion.24
  148.0 1.8 copy.43
  149.8 24.8 %all-to-all-start.1 = ((bf16[16,16,1,4,448]{4,3,1,2,0:T(4,128)(2,1)}), bf16[16,16,1,4,448]{4,3,1,2,0:T(4,128)(2,1)S(1)}, u32[]{:S(2)}, u32[]{:S(2)}) async-start(bf16[16,16,1,4,448]{4,3,1,2,0:T(4,128)(2,1)} %copy.43), calls=%async_computation.1 | async-start | bytes 2097152 | tf_op jit(solution)/shard_map/all_to_all | solution.py:37
  174.7 27.0 %all-to-all-done.1 = bf16[16,16,1,4,448]{4,3,1,2,0:T(4,128)(2,1)S(1)} async-done(((bf16[16,16,1,4,448]{4,3,1,2,0:T(4,128)(2,1)}), bf16[16,16,1,4,448]{4,3,1,2,0:T(4,128)(2,1)S(1)}, u32[]{:S(2)}, u32[]{:S(2)}) %all-to-all-start.1) | async-done | bytes 917536 | tf_op jit(solution)/shard_map/all_to_all | solution.py:37
  201.7 1.1 reduce_sum.92
  202.8 5.3 all-to-all-start.2
  208.6 9.2 %all-to-all-done.2 = bf16[16,1,4,448]{3,2,1,0:T(4,128)(2,1)S(1)} async-done(((bf16[16,1,4,448]{3,2,1,0:T(4,128)(2,1)}), bf16[16,1,4,448]{3,2,1,0:T(4,128)(2,1)S(1)}, u32[]{:S(2)}, u32[]{:S(2)}) %all-to-all-start.2) | async-done | bytes 57376 | tf_op jit(solution)/shard_map/all_to_all | solution.py:136
  218.3 0.6 copy-done.5
  219.8 27.5 %all_to_all.47 = bf16[16,3,7168]{2,1,0:T(4,128)(2,1)} all-to-all(bf16[16,3,7168]{2,1,0:T(4,128)(2,1)S(1)} %reshape.337), channel_id=1, replica_groups=mesh['ctx'=16,'exp'=16] {'exp'}, dimensions={0} | all-to-all | bytes 1376256 | tf_op jit(solution)/shard_map/all_to_all | solution.py:161
  247.3 2.3 all_to_all.37
  249.7 122.6 %all-gather.5.cloned.1.call-done = bf16[1,768,7168]{2,1,0:T(8,128)(2,1)} async-done(((bf16[1,48,7168]{2,1,0:T(8,128)(2,1)}), bf16[1,768,7168]{2,1,0:T(8,128)(2,1)}) %all-gather.5.cloned.1.call-update) | async-done | bytes 11010064 | tf_op jit(solution)/shard_map/all_gather | solution.py:169
  372.3 6.3 %fusion.2 = f32[768,128]{1,0:T(8,128)S(1)} fusion(bf16[1,768,7168]{2,1,0:T(8,128)(2,1)} %all-gather.5.cloned.1.call-done, bf16[1,7168,128]{2,1,0:T(8,128)(2,1)} %param.25), kind=kOutput, calls=%fused_computation.3 | convolution fusion | flops 1409286144 | bytes 13238272 | tf_op jit(solution)/shard_map/end,edf->enf/dot_general | solution.py:170
  378.7 17.3 %fusion.4 = bf16[768,1,7168]{2,0,1:T(8,128)(2,1)} fusion(bf16[1,128,7168]{2,1,0:T(8,128)(2,1)S(1)} %copy-done, bf16[1,7168,128]{2,1,0:T(8,128)(2,1)} %param.26, bf16[1,768,7168]{2,1,0:T(8,128)(2,1)} %all-gather.5.cloned.1.call-done, f32[768,128]{1,0:T(8,128)S(1)} %fusion.2), kind=kOutput, calls=%fused_computation.5 | convolution fusion | flops 2824667136 | bytes 26083328 | tf_op jit(solution)/shard_map/enf,efd->ned/dot_general | solution.py:174
  396.0 155.5 %reduce-scatter.2.cloned.1.call-done = bf16[48,1,7168]{2,0,1:T(8,128)(2,1)} async-done(((bf16[768,1,7168]{2,0,1:T(8,128)(2,1)}), bf16[48,1,7168]{2,0,1:T(8,128)(2,1)}) %reduce-scatter.2.cloned.1.call-update) | async-done | bytes 688144 | tf_op jit(solution)/shard_map/reduce_scatter | solution.py:173
  551.5 2.2 reshape.342
  553.7 4.5 all-to-all-start.4
  558.9 23.5 %all-to-all-done.4 = bf16[16,3,1,7168]{3,1,2,0:T(4,128)(2,1)S(1)} async-done(((bf16[16,3,1,7168]{3,1,2,0:T(4,128)(2,1)}), bf16[16,3,1,7168]{3,1,2,0:T(4,128)(2,1)S(1)}, u32[]{:S(2)}, u32[]{:S(2)}) %all-to-all-start.4) | async-done | bytes 688160 | tf_op jit(solution)/shard_map/all_to_all | solution.py:182
  582.7 1.0 fusion.5
  (74 shorter events, 3.8 us)
Async XLA Ops:
  6.5 372.1 %copy-start = (bf16[1,128,7168]{2,1,0:T(8,128)(2,1)S(1)}, bf16[1,128,7168]{2,1,0:T(8,128)(2,1)}, u32[]{:S(2)}) copy-start(bf16[1,128,7168]{2,1,0:T(8,128)(2,1)} %param.27) | copy-start | bytes 5505028
  6.5 83.3 %all-gather.3.cloned.1.call-start = ((), (), s32[]{:S(2)}) async-start(), calls=%async_computation.6 | async-start | bytes 4177920 | tf_op jit(solution)/shard_map/all_gather | solution.py:118
  96.8 2.7 copy-start.1
  100.8 5.7 copy-start.2
  107.9 38.5 %copy-start.14 = (bf16[1024,448]{0,1:T(8,128)(2,1)S(1)}, bf16[1024,448]{0,1:T(8,128)(2,1)}, u32[]{:S(2)}) copy-start(bf16[1024,448]{0,1:T(8,128)(2,1)} %param.20) | copy-start | bytes 2752516
  147.9 26.7 %copy-start.12 = (s32[4,8]{1,0:T(4,128)S(1)}, s32[4,8]{1,0:T(4,128)}, u32[]{:S(2)}) copy-start(s32[4,8]{1,0:T(4,128)} %param.24) | copy-start | bytes 388
  147.9 70.1 %copy-start.3 = (bf16[4,7168]{1,0:T(4,128)(2,1)S(1)}, bf16[4,7168]{1,0:T(4,128)(2,1)}, u32[]{:S(2)}) copy-start(bf16[4,7168]{1,0:T(4,128)(2,1)} %param.21) | copy-start | bytes 172036
  147.9 70.3 %copy-start.9 = (f32[7168]{0:T(1024)S(1)}, f32[7168]{0:T(1024)}, u32[]{:S(2)}) copy-start(f32[7168]{0:T(1024)} %param.22) | copy-start | bytes 86020
  149.8 51.9 %all-to-all-start.1 = ((bf16[16,16,1,4,448]{4,3,1,2,0:T(4,128)(2,1)}), bf16[16,16,1,4,448]{4,3,1,2,0:T(4,128)(2,1)S(1)}, u32[]{:S(2)}, u32[]{:S(2)}) async-start(bf16[16,16,1,4,448]{4,3,1,2,0:T(4,128)(2,1)} %copy.43), calls=%async_computation.1 | async-start | bytes 2097152 | tf_op jit(solution)/shard_map/all_to_all | solution.py:37
  174.7 43.5 %copy-start.7 = (s32[4,16]{1,0:T(4,128)}, s32[4,16]{1,0:T(4,128)S(1)}, u32[]{:S(2)}) copy-start(s32[4,16]{1,0:T(4,128)S(1)} %convert_reduce_fusion) | copy-start | bytes 772
  202.8 15.0 %all-to-all-start.2 = ((bf16[16,1,4,448]{3,2,1,0:T(4,128)(2,1)}), bf16[16,1,4,448]{3,2,1,0:T(4,128)(2,1)S(1)}, u32[]{:S(2)}, u32[]{:S(2)}) async-start(bf16[16,1,4,448]{3,2,1,0:T(4,128)(2,1)} %bitcast.12), calls=%async_computation.2 | async-start | bytes 131072 | tf_op jit(solution)/shard_map/all_to_all | solution.py:136
  208.1 164.3 %all-gather.5.cloned.1.call-start = ((), (), s32[]{:S(2)}) async-start(), calls=%async_computation.7 | async-start | bytes 11698176 | tf_op jit(solution)/shard_map/all_gather | solution.py:169
  208.2 9.6 %copy-start.10 = (s32[4,16]{1,0:T(4,128)}, s32[4,16]{1,0:T(4,128)S(1)}, u32[]{:S(2)}) copy-start(s32[4,16]{1,0:T(4,128)S(1)} %sub.74) | copy-start | bytes 772
  218.3 0.6 copy-start.5
  249.7 301.8 %reduce-scatter.2.cloned.1.call-start = ((), (), s32[]{:S(2)}) async-start(), calls=%async_computation.8 | async-start | bytes 11698176 | tf_op jit(solution)/shard_map/reduce_scatter | solution.py:173
  396.0 162.2 %copy-start.8 = (s32[4,16]{1,0:T(4,128)S(1)}, s32[4,16]{1,0:T(4,128)}, u32[]{:S(2)}) copy-start(s32[4,16]{1,0:T(4,128)} %copy-done.7) | copy-start | bytes 772
  396.0 162.3 %copy-start.6 = (bf16[4,7168]{1,0:T(4,128)(2,1)S(1)}, bf16[4,7168]{1,0:T(4,128)(2,1)}, u32[]{:S(2)}) copy-start(bf16[4,7168]{1,0:T(4,128)(2,1)} %copy-done.5) | copy-start | bytes 172036
  396.0 162.3 %copy-start.15 = (bf16[7168,16]{0,1:T(8,128)(2,1)S(1)}, bf16[7168,16]{0,1:T(8,128)(2,1)}, u32[]{:S(2)}) copy-start(bf16[7168,16]{0,1:T(8,128)(2,1)} %param.23) | copy-start | bytes 688132
  396.0 162.5 %copy-start.13 = (s32[4,8]{1,0:T(4,128)S(1)}, s32[4,8]{1,0:T(4,128)}, u32[]{:S(2)}) copy-start(s32[4,8]{1,0:T(4,128)} %param.24) | copy-start | bytes 388
  396.0 162.8 %copy-start.11 = (s32[4,16]{1,0:T(4,128)S(1)}, s32[4,16]{1,0:T(4,128)}, u32[]{:S(2)}) copy-start(s32[4,16]{1,0:T(4,128)} %copy-done.10) | copy-start | bytes 772
  396.0 186.6 %copy-start.4 = (bf16[4,7168]{1,0:T(4,128)(2,1)S(1)}, bf16[4,7168]{1,0:T(4,128)(2,1)}, u32[]{:S(2)}) copy-start(bf16[4,7168]{1,0:T(4,128)(2,1)} %param.21) | copy-start | bytes 172036
  553.7 28.7 %all-to-all-start.4 = ((bf16[16,3,1,7168]{3,1,2,0:T(4,128)(2,1)}), bf16[16,3,1,7168]{3,1,2,0:T(4,128)(2,1)S(1)}, u32[]{:S(2)}, u32[]{:S(2)}) async-start(bf16[16,3,1,7168]{3,1,2,0:T(4,128)(2,1)} %bitcast.106), calls=%async_computation.5 | async-start | bytes 1835008 | tf_op jit(solution)/shard_map/all_to_all | solution.py:182
Sparse Core Ops, SparseCore 0:
  10.0 79.7 all-gather.2
  249.8 122.4 all-gather.4
  396.1 155.3 reduce-scatter.1
where the time goes:
time: 591 us; the launch traced here: 590 us
  waiting for transfers between devices  415 us (70%)
  blocking collectives  64.9 us (11%)
  matrix products  40.4 us (7%)
  starting transfers between devices  34.7 us (6%)
  local copies, waits for them, and re-layouts  14.9 us (3%)
  between operations  13.5 us (2%)
  other arithmetic  6.29 us (1%)
    reduce_scatter x1, waiting for transfers between devices, body(): lax.psum_scatter(jnp.einsum('enf,efd->ned', activations, w_down, preferre...  155 us
    all_gather x1, waiting for transfers between devices, body(): portion = lax.all_gather(arrived, 'ctx', axis=1, tiled=True)  123 us
    all_gather x1, waiting for transfers between devices, body(): portion = lax.all_gather(keys_here, 'ctx', axis=1, tiled=True)  77.7 us
    all_to_all x1, blocking collectives, copy_for_each(): return lax.all_to_all(copies, axis, split_axis=0, concat_axis=0, tiled=True)  37.4 us
    all_to_all x1, blocking collectives, body(): lax.all_to_all(send_rows.reshape(expert_count, CAP, model_width), 'exp',...  27.5 us
    all_to_all x1, waiting for transfers between devices, sum_at_owner(): lax.all_to_all(in_blocks(value, dim, length), axis, 0, 0, tiled=True)  27 us
    all_to_all x1, starting transfers between devices, sum_at_owner(): lax.all_to_all(in_blocks(value, dim, length), axis, 0, 0, tiled=True)  24.8 us
    all_to_all x1, waiting for transfers between devices, body(): lax.all_to_all(going_back, 'exp', split_axis=0, concat_axis=2, tiled=True)  23.5 us
  transfers between devices with their start and end apart: 6, of which 6 were waited for; matrix products, arithmetic and copies ran while one was open for 1% of the time, Pallas kernels for 0%

commit v1 on v0

--- a/solution.py
+++ b/solution.py
@@ -166,7 +166,9 @@
         tiled=True,
     )
     local_experts = arrived.shape[0]
-    portion = lax.all_gather(arrived, "ctx", axis=1, tiled=True)
+    portion = jnp.concatenate(
+        lax.all_to_all(jnp.stack([arrived] * lax.axis_size("ctx")), "ctx", 0, 0), axis=1
+    )
     gate = jnp.einsum("end,edf->enf", portion, w_gate, preferred_element_type=jnp.float32)
     upward = jnp.einsum("end,edf->enf", portion, w_up, preferred_element_type=jnp.float32)
     activations = (jax.nn.silu(gate) * upward).astype(jnp.bfloat16)

time: 591 us -> 724 us (1.23)
  blocking collectives: 64.9 us -> 313 us
  waiting for transfers between devices: 415 us -> 295 us
  local copies, waits for them, and re-layouts: 14.9 us -> 23.8 us
    all_to_all x0 -> x1, blocking collectives: none -> 248 us  [body(): lax.all_to_all(jnp.stack([arrived] * lax.axis_size('ctx')), 'ctx', 0, 0)]
    all_gather x1 -> x0, waiting for transfers between devices: 123 us -> none  [body(): portion = lax.all_gather(arrived, 'ctx', axis=1, tiled=True)]
  transfers between devices with their start and end apart: 6 -> 5, of which waited for: 6 -> 5; matrix products, arithmetic and copies ran while one was open for 1% -> 1% of each run, Pallas kernels for 0% -> 0%
where the time goes in v1:
time: 724 us
  blocking collectives  313 us (43%)
  waiting for transfers between devices  295 us (41%)
  matrix products  37.2 us (5%)
  starting transfers between devices  34.7 us (5%)
  local copies, waits for them, and re-layouts  23.8 us (3%)
  between operations  13.8 us (2%)
    all_to_all x1, blocking collectives, body(): lax.all_to_all(jnp.stack([arrived] * lax.axis_size('ctx')), 'ctx', 0, 0)  248 us
    reduce_scatter x1, waiting for transfers between devices, body(): lax.psum_scatter(jnp.einsum('enf,efd->ned', activations, w_down, preferre...  157 us
    all_gather x1, waiting for transfers between devices, body(): portion = lax.all_gather(keys_here, 'ctx', axis=1, tiled=True)  77.7 us
    all_to_all x1, blocking collectives, copy_for_each(): return lax.all_to_all(copies, axis, split_axis=0, concat_axis=0, tiled=True)  37.4 us
    all_to_all x1, blocking collectives, body(): lax.all_to_all(send_rows.reshape(expert_count, CAP, model_width), 'exp',...  27.5 us
    all_to_all x1, waiting for transfers between devices, sum_at_owner(): lax.all_to_all(in_blocks(value, dim, length), axis, 0, 0, tiled=True)  27 us
    all_to_all x1, starting transfers between devices, sum_at_owner(): lax.all_to_all(in_blocks(value, dim, length), axis, 0, 0, tiled=True)  24.8 us
    all_to_all x1, waiting for transfers between devices, body(): lax.all_to_all(going_back, 'exp', split_axis=0, concat_axis=2, tiled=True)  23.5 us
  transfers between devices with their start and end apart: 5, of which 5 were waited for; matrix products, arithmetic and copies ran while one was open for 1% of the time, Pallas kernels for 0%

profile of v1, /device:TPU:1, one launch (start us, length us, event | category | flops | bytes accessed | tf_op | source)
XLA Modules:
  0.0 723.8 jit_solution(2725896101966155431)
XLA Ops:
  6.5 1.2 copy.37
  7.7 1.6 pad_maximum_fusion
  9.4 1.0 reshape.342
  11.1 0.8 select_reduce_fusion
  12.2 77.7 %all-gather.2.cloned.1.call-done = bf16[576,3072]{0,1:T(8,128)(2,1)} async-done(((bf16[576,192]{0,1:T(8,128)(2,1)}), bf16[576,3072]{0,1:T(8,128)(2,1)}) %all-gather.2.cloned.1.call-update) | async-done | bytes 3538960 | tf_op jit(solution)/shard_map/all_gather | solution.py:118
  89.8 3.9 fusion.9
  93.7 3.1 fusion.82
  96.8 2.6 copy-done.2
  99.5 1.0 fusion.2
  100.8 5.6 fusion.35
  106.4 1.2 fusion.48
  108.0 37.4 %all_to_all.48 = bf16[16,64,1024]{2,1,0:T(8,128)(2,1)S(1)} all-to-all(bf16[16,64,1024]{2,1,0:T(8,128)(2,1)S(1)} %broadcast_in_dim.120), channel_id=1, replica_groups=mesh['ctx'=16,'exp'=16] {'ctx'}, dimensions={0} | all-to-all | bytes 4194304 | tf_op jit(solution)/shard_map/all_to_all | solution.py:15
  145.3 1.2 copy.41
  146.5 1.4 fusion.22
  148.0 1.8 copy.43
  149.8 24.8 %all-to-all-start.1 = ((bf16[16,16,1,4,448]{4,3,1,2,0:T(4,128)(2,1)}), bf16[16,16,1,4,448]{4,3,1,2,0:T(4,128)(2,1)S(1)}, u32[]{:S(2)}, u32[]{:S(2)}) async-start(bf16[16,16,1,4,448]{4,3,1,2,0:T(4,128)(2,1)} %copy.43), calls=%async_computation.1 | async-start | bytes 2097152 | tf_op jit(solution)/shard_map/all_to_all | solution.py:37
  174.7 27.0 %all-to-all-done.1 = bf16[16,16,1,4,448]{4,3,1,2,0:T(4,128)(2,1)S(1)} async-done(((bf16[16,16,1,4,448]{4,3,1,2,0:T(4,128)(2,1)}), bf16[16,16,1,4,448]{4,3,1,2,0:T(4,128)(2,1)S(1)}, u32[]{:S(2)}, u32[]{:S(2)}) %all-to-all-start.1) | async-done | bytes 917536 | tf_op jit(solution)/shard_map/all_to_all | solution.py:37
  201.7 1.1 reduce_sum.92
  202.8 5.3 all-to-all-start.2
  208.6 9.2 %all-to-all-done.2 = bf16[16,1,4,448]{3,2,1,0:T(4,128)(2,1)S(1)} async-done(((bf16[16,1,4,448]{3,2,1,0:T(4,128)(2,1)}), bf16[16,1,4,448]{3,2,1,0:T(4,128)(2,1)S(1)}, u32[]{:S(2)}, u32[]{:S(2)}) %all-to-all-start.2) | async-done | bytes 57376 | tf_op jit(solution)/shard_map/all_to_all | solution.py:136
  219.8 27.5 %all_to_all.49 = bf16[16,3,7168]{2,1,0:T(4,128)(2,1)} all-to-all(bf16[16,3,7168]{2,1,0:T(4,128)(2,1)S(1)} %reshape.345), channel_id=1, replica_groups=mesh['ctx'=16,'exp'=16] {'exp'}, dimensions={0} | all-to-all | bytes 1376256 | tf_op jit(solution)/shard_map/all_to_all | solution.py:161
  247.3 1.6 stack.4
  249.0 5.5 stack.5
  254.5 248.3 %all_to_all.50 = bf16[16,1,48,7168]{3,2,1,0:T(8,128)(2,1)S(1)} all-to-all(bf16[16,1,48,7168]{3,2,1,0:T(8,128)(2,1)} %stack.5), channel_id=1, replica_groups=mesh['ctx'=16,'exp'=16] {'ctx'}, dimensions={0} | all-to-all | bytes 22020096 | tf_op jit(solution)/shard_map/all_to_all | solution.py:170
  502.8 4.0 copy-done.1
  506.9 3.0 fusion.17
  509.9 17.3 %fusion = bf16[768,1,7168]{2,0,1:T(8,128)(2,1)} fusion(bf16[1,128,7168]{2,1,0:T(8,128)(2,1)S(1)} %copy-done, bf16[768,7168]{1,0:T(8,128)(2,1)} %bitcast.99, bf16[1,7168,128]{2,1,0:T(8,128)(2,1)} %param.26, f32[768,128]{1,0:T(8,128)S(1)} %fusion.17), kind=kOutput, calls=%fused_computation.1 | convolution fusion | flops 2824667136 | bytes 26083328 | tf_op jit(solution)/shard_map/enf,efd->ned/dot_general | solution.py:176
  527.3 157.5 %reduce-scatter.2.cloned.1.call-done = bf16[48,1,7168]{2,0,1:T(8,128)(2,1)} async-done(((bf16[768,1,7168]{2,0,1:T(8,128)(2,1)}), bf16[48,1,7168]{2,0,1:T(8,128)(2,1)}) %reduce-scatter.2.cloned.1.call-update) | async-done | bytes 688144 | tf_op jit(solution)/shard_map/reduce_scatter | solution.py:175
  684.8 2.2 reshape.350
  687.0 4.5 all-to-all-start.5
  692.2 23.5 %all-to-all-done.5 = bf16[16,3,1,7168]{3,1,2,0:T(4,128)(2,1)S(1)} async-done(((bf16[16,3,1,7168]{3,1,2,0:T(4,128)(2,1)}), bf16[16,3,1,7168]{3,1,2,0:T(4,128)(2,1)S(1)}, u32[]{:S(2)}, u32[]{:S(2)}) %all-to-all-start.5) | async-done | bytes 688160 | tf_op jit(solution)/shard_map/all_to_all | solution.py:184
  716.0 1.0 fusion.1
  (77 shorter events, 5.1 us)
Async XLA Ops:
  6.5 503.3 %copy-start = (bf16[1,128,7168]{2,1,0:T(8,128)(2,1)S(1)}, bf16[1,128,7168]{2,1,0:T(8,128)(2,1)}, u32[]{:S(2)}) copy-start(bf16[1,128,7168]{2,1,0:T(8,128)(2,1)} %param.27) | copy-start | bytes 5505028
  6.5 83.3 %all-gather.2.cloned.1.call-start = ((), (), s32[]{:S(2)}) async-start(), calls=%async_computation.7 | async-start | bytes 4177920 | tf_op jit(solution)/shard_map/all_gather | solution.py:118
  96.8 2.7 copy-start.2
  100.8 5.7 copy-start.3
  107.9 38.5 %copy-start.16 = (bf16[1024,448]{0,1:T(8,128)(2,1)S(1)}, bf16[1024,448]{0,1:T(8,128)(2,1)}, u32[]{:S(2)}) copy-start(bf16[1024,448]{0,1:T(8,128)(2,1)} %param.20) | copy-start | bytes 2752516
  147.9 26.7 %copy-start.13 = (s32[4,8]{1,0:T(4,128)S(1)}, s32[4,8]{1,0:T(4,128)}, u32[]{:S(2)}) copy-start(s32[4,8]{1,0:T(4,128)} %param.24) | copy-start | bytes 388
  147.9 70.1 %copy-start.4 = (bf16[4,7168]{1,0:T(4,128)(2,1)S(1)}, bf16[4,7168]{1,0:T(4,128)(2,1)}, u32[]{:S(2)}) copy-start(bf16[4,7168]{1,0:T(4,128)(2,1)} %param.21) | copy-start | bytes 172036
  147.9 70.3 %copy-start.10 = (f32[7168]{0:T(1024)S(1)}, f32[7168]{0:T(1024)}, u32[]{:S(2)}) copy-start(f32[7168]{0:T(1024)} %param.22) | copy-start | bytes 86020
  149.8 51.9 %all-to-all-start.1 = ((bf16[16,16,1,4,448]{4,3,1,2,0:T(4,128)(2,1)}), bf16[16,16,1,4,448]{4,3,1,2,0:T(4,128)(2,1)S(1)}, u32[]{:S(2)}, u32[]{:S(2)}) async-start(bf16[16,16,1,4,448]{4,3,1,2,0:T(4,128)(2,1)} %copy.43), calls=%async_computation.1 | async-start | bytes 2097152 | tf_op jit(solution)/shard_map/all_to_all | solution.py:37
  174.7 43.5 %copy-start.8 = (s32[4,16]{1,0:T(4,128)}, s32[4,16]{1,0:T(4,128)S(1)}, u32[]{:S(2)}) copy-start(s32[4,16]{1,0:T(4,128)S(1)} %convert_reduce_fusion) | copy-start | bytes 772
  202.8 15.0 %all-to-all-start.2 = ((bf16[16,1,4,448]{3,2,1,0:T(4,128)(2,1)}), bf16[16,1,4,448]{3,2,1,0:T(4,128)(2,1)S(1)}, u32[]{:S(2)}, u32[]{:S(2)}) async-start(bf16[16,1,4,448]{3,2,1,0:T(4,128)(2,1)} %bitcast.12), calls=%async_computation.2 | async-start | bytes 131072 | tf_op jit(solution)/shard_map/all_to_all | solution.py:136
  208.1 476.7 %reduce-scatter.2.cloned.1.call-start = ((), (), s32[]{:S(2)}) async-start(), calls=%async_computation.8 | async-start | bytes 11698176 | tf_op jit(solution)/shard_map/reduce_scatter | solution.py:175
  208.2 9.6 %copy-start.11 = (s32[4,16]{1,0:T(4,128)}, s32[4,16]{1,0:T(4,128)S(1)}, u32[]{:S(2)}) copy-start(s32[4,16]{1,0:T(4,128)S(1)} %sub.74) | copy-start | bytes 772
  218.3 0.6 copy-start.6
  254.5 252.4 %copy-start.15 = (bf16[1,7168,128]{2,1,0:T(8,128)(2,1)S(1)}, bf16[1,7168,128]{2,1,0:T(8,128)(2,1)}, u32[]{:S(2)}) copy-start(bf16[1,7168,128]{2,1,0:T(8,128)(2,1)} %param.25) | copy-start | bytes 5505028
  502.8 4.0 copy-start.1
  527.2 164.3 %copy-start.9 = (s32[4,16]{1,0:T(4,128)S(1)}, s32[4,16]{1,0:T(4,128)}, u32[]{:S(2)}) copy-start(s32[4,16]{1,0:T(4,128)} %copy-done.8) | copy-start | bytes 772
  527.2 164.3 %copy-start.7 = (bf16[4,7168]{1,0:T(4,128)(2,1)S(1)}, bf16[4,7168]{1,0:T(4,128)(2,1)}, u32[]{:S(2)}) copy-start(bf16[4,7168]{1,0:T(4,128)(2,1)} %copy-done.6) | copy-start | bytes 172036
  527.2 164.3 %copy-start.17 = (bf16[7168,16]{0,1:T(8,128)(2,1)S(1)}, bf16[7168,16]{0,1:T(8,128)(2,1)}, u32[]{:S(2)}) copy-start(bf16[7168,16]{0,1:T(8,128)(2,1)} %param.23) | copy-start | bytes 688132
  527.2 164.5 %copy-start.14 = (s32[4,8]{1,0:T(4,128)S(1)}, s32[4,8]{1,0:T(4,128)}, u32[]{:S(2)}) copy-start(s32[4,8]{1,0:T(4,128)} %param.24) | copy-start | bytes 388
  527.2 164.8 %copy-start.12 = (s32[4,16]{1,0:T(4,128)S(1)}, s32[4,16]{1,0:T(4,128)}, u32[]{:S(2)}) copy-start(s32[4,16]{1,0:T(4,128)} %copy-done.11) | copy-start | bytes 772
  527.3 188.7 %copy-start.5 = (bf16[4,7168]{1,0:T(4,128)(2,1)S(1)}, bf16[4,7168]{1,0:T(4,128)(2,1)}, u32[]{:S(2)}) copy-start(bf16[4,7168]{1,0:T(4,128)(2,1)} %param.21) | copy-start | bytes 172036
  687.0 28.7 %all-to-all-start.5 = ((bf16[16,3,1,7168]{3,1,2,0:T(4,128)(2,1)}), bf16[16,3,1,7168]{3,1,2,0:T(4,128)(2,1)S(1)}, u32[]{:S(2)}, u32[]{:S(2)}) async-start(bf16[16,3,1,7168]{3,1,2,0:T(4,128)(2,1)} %bitcast.100), calls=%async_computation.6 | async-start | bytes 1835008 | tf_op jit(solution)/shard_map/all_to_all | solution.py:184
Sparse Core Ops, SparseCore 0:
  10.0 79.7 all-gather.1
  527.4 157.3 reduce-scatter.1
